TPU v7x, 32 devices: a whole 2x2x4 slice. The times are simulated.
32 devices in a mesh: fsdp: 8 (over z, x), dp: 4 (over y, core).
Axes of the slice: x: 2, y: 2, z: 4, core: 2. Of those that a mesh axis runs over, the one named last changes fastest.
Arguments:
- features: bfloat16 [8192, 1024], P(('fsdp', 'dp')), may hold values from -6 to 6
- normed: bfloat16 [8192, 4096], P(('fsdp', 'dp')), may hold values from -6 to 6
- relu_mask: int32 [8192, 4096], P(('fsdp', 'dp')), may hold values 0 or 1
- cotangent: bfloat16 [8192, 4096], P(('fsdp', 'dp')), may hold values from -40 to 40
- weight_shard: bfloat16 [1024, 4096], P('fsdp'), may hold values from -0.1875 to 0.1875
- norm_gain: float32 [4096], replicated, may hold values from 0.25 to 1.75
- inverse_deviation: float32 [4096], replicated, may hold values from 0.5 to 3
Outputs:
- grad_input: bfloat16 [8192, 1024], P(('fsdp', 'dp'))
- grad_weight: float32 [1024, 4096], P('fsdp')
- grad_gain: float32 [4096], replicated
- grad_shift: float32 [4096], replicated
All inputs are finite; a program needn't handle non-finite values. No bound on the sum of `relu_mask` on one device may be relied on, other than what follows from the above.
Results may differ from a plain program's by a relative error of at most 0.005.
Values may be sent and summed in bfloat16 or wider, within the bound.
No kernel may reach another device: no remote copies, remote signals or barrier semaphores. Data moves between devices by JAX's collectives and lax.ppermute only.
A program may use at most 128 MiB of HBM per device.

v0:
```python
import math
import jax
import jax.numpy as jnp
from jax import lax
from jax.sharding import PartitionSpec as P


def on_device(features, normed, relu_mask, cotangent, weight_shard, norm_gain, inverse_deviation):
    local_rows = features.shape[0]
    total_rows = local_rows * lax.axis_size("fsdp") * lax.axis_size("dp")
    masked = cotangent.astype(jnp.float32) * relu_mask.astype(jnp.float32)
    normed_f = normed.astype(jnp.float32)
    local_plain = jnp.sum(masked, axis=0)
    local_cross = jnp.sum(masked * normed_f, axis=0)
    sum_plain, sum_cross = lax.psum((local_plain, local_cross), ("fsdp", "dp"))
    norm_grad = (
        inverse_deviation
        * norm_gain
        * (masked - sum_plain / total_rows - normed_f * (sum_cross / total_rows))
    )
    norm_grad = norm_grad.astype(jnp.bfloat16)
    grad_input = lax.dot_general(
        norm_grad,
        lax.all_gather(weight_shard, "fsdp", axis=0, tiled=True),
        (((1,), (1,)), ((), ())),
        preferred_element_type=jnp.float32,
    ).astype(jnp.bfloat16)
    unit_block = lax.all_to_all(norm_grad, "dp", split_axis=1, concat_axis=0, tiled=True)
    unit_term = lax.dot_general(
        lax.all_gather(features, "dp", axis=0, tiled=True),
        unit_block,
        (((0,), (0,)), ((), ())),
        preferred_element_type=jnp.float32,
    )
    owner_part = lax.psum_scatter(unit_term, "fsdp", scatter_dimension=0, tiled=True)
    summed = lax.all_gather(owner_part, "dp", axis=1, tiled=True)
    rescale = 1.0 / math.sqrt(total_rows)
    return (grad_input, summed * rescale, sum_cross * rescale, sum_plain * rescale)


def solution(mesh):
    in_specs = (
        P(("fsdp", "dp"), None),
        P(("fsdp", "dp"), None),
        P(("fsdp", "dp"), None),
        P(("fsdp", "dp"), None),
        P("fsdp", None),
        P(),
        P(),
    )
    out_specs = (P(("fsdp", "dp"), None), P("fsdp", None), P(), P())
    return jax.shard_map(
        on_device, mesh=mesh, in_specs=in_specs, out_specs=out_specs, check_vma=False
    )
```

profile of v0, /device:TPU:0, one launch (start us, length us, event | category | flops | bytes accessed | tf_op | source)
XLA Modules:
  0.0 361.4 jit_solution(14963796621022647305)
XLA Ops:
  7.2 0.0 all-gather.6.cloned.1.call-start
  7.2 0.7 all-gather.6.cloned.1.call-update
  7.9 0.0 reduce-scatter.2.cloned.1.call-start
  7.9 3.3 copy.15
  11.2 5.6 %copy.14 = s32[256,4096]{0,1:T(8,128)} copy(s32[256,4096]{1,0:T(8,128)} %param.9) | data formatting | bytes 8388608 | tf_op args[2]
  16.8 4.1 %copy.13 = bf16[256,4096]{0,1:T(8,128)(2,1)} copy(bf16[256,4096]{1,0:T(8,128)(2,1)} %param.10) | data formatting | bytes 4194304 | tf_op args[3]
  21.0 0.0 copy-start.2
  21.0 0.0 copy-start.3
  21.0 4.1 %fusion.4 = (f32[4096]{0:T(1024)S(1)}, f32[4096]{0:T(1024)S(1)}) fusion(s32[256,4096]{0,1:T(8,128)} %copy.14, bf16[256,4096]{0,1:T(8,128)(2,1)} %copy.13, bf16[256,4096]{0,1:T(8,128)(2,1)S(1)} %copy.15), kind=kLoop, calls=%fused_computation.8 | loop fusion | flops 7331840 | bytes 8421376 | tf_op jit(solution)/shard_map/reduce_sum | solution.py:13
  25.1 0.0 copy-done.2
  25.1 0.0 copy-done.3
  25.1 42.3 %all-reduce = (f32[4096]{0:T(1024)S(1)}, f32[4096]{0:T(1024)S(1)}) all-reduce(f32[4096]{0:T(1024)S(1)} %get-tuple-element.17, f32[4096]{0:T(1024)S(1)} %get-tuple-element.16), channel_id=1, replica_groups=mesh['fsdp'=8,'dp'=4] {'fsdp','dp'}, use_global_device_ids=true, to_apply=%region_3.0 | all-reduce | flops 8192 | bytes 65536 | tf_op jit(solution)/shard_map/psum | solution.py:15
  67.4 0.6 broadcast_multiply_fusion.1
  68.0 4.3 %fusion.3 = bf16[256,4096]{0,1:T(8,128)(2,1)S(1)} fusion(bf16[256,4096]{0,1:T(8,128)(2,1)S(1)} %copy.15, f32[4096]{0:T(1024)S(1)} %get-tuple-element.24, f32[4096]{0:T(1024)S(1)} %get-tuple-element.21, f32[4096]{0:T(1024)S(1)} %mul.37, s32[256,4096]{0,1:T(8,128)} %copy.14, bf16[256,4096]{0,1:T(8,128)(2,1)} %copy.13), kind=kLoop, calls=%fused_computation.5 | loop fusion | flops 9437184 | bytes 10534912 | tf_op jit(solution)/shard_map/convert_element_type | solution.py:21
  72.3 0.0 copy-start
  72.3 29.0 %all_to_all.19 = bf16[256,4,1024]{0,2,1:T(8,128)(2,1)S(1)} all-to-all(bf16[256,4,1024]{0,2,1:T(8,128)(2,1)S(1)} %bitcast.9), channel_id=1, replica_groups=mesh['fsdp'=8,'dp'=4] {'dp'}, dimensions={1} | all-to-all | bytes 4194304 | tf_op jit(solution)/shard_map/all_to_all | solution.py:28
  101.3 0.0 copy-done
  101.3 2.4 copy.16
  103.7 0.0 all-gather.6.cloned.1.call-done
  103.7 6.5 %convolution_bitcast_fusion = f32[1024,1024]{0,1:T(8,128)} fusion(bf16[1024,1024]{1,0:T(8,128)(2,1)} %bitcast.11, bf16[1024,1024]{1,0:T(8,128)(2,1)} %all-gather.6.cloned.1.call-done), kind=kOutput, calls=%fused_computation.7 | convolution fusion | flops 2147483648 | bytes 8388608 | tf_op jit(solution)/shard_map/dot_general | solution.py:29
  110.3 0.0 reduce-scatter.2.cloned.1.call-update
  110.3 0.0 all-gather.8.cloned.1.call-start
  110.3 87.7 %reduce-scatter.2.cloned.1.call-done = f32[128,1024]{0,1:T(8,128)} async-done(((f32[1024,1024]{0,1:T(8,128)}), f32[128,1024]{0,1:T(8,128)}) %reduce-scatter.2.cloned.1.call-update) | async-done | bytes 524304 | tf_op jit(solution)/shard_map/reduce_scatter | solution.py:35
  198.0 0.0 all-gather.8.cloned.1.call-update
  198.1 0.0 all-gather.4.cloned.1.call-start
  198.1 0.5 all-gather.4.cloned.1.call-update
  198.6 23.2 %all-gather.8.cloned.1.call-done = f32[128,4096]{0,1:T(8,128)} async-done(((f32[128,1024]{0,1:T(8,128)}), f32[128,4096]{0,1:T(8,128)}) %all-gather.8.cloned.1.call-update) | async-done | bytes 2097168 | tf_op jit(solution)/shard_map/all_gather | solution.py:36
  221.8 3.1 broadcast_multiply_fusion
  224.9 0.0 copy-start.1
  224.9 3.0 copy.17
  227.9 120.4 %all-gather.4.cloned.1.call-done = bf16[1024,4096]{1,0:T(8,128)(2,1)} async-done(((bf16[128,4096]{1,0:T(8,128)(2,1)}), bf16[1024,4096]{1,0:T(8,128)(2,1)}) %all-gather.4.cloned.1.call-update) | async-done | bytes 8388624 | tf_op jit(solution)/shard_map/all_gather | solution.py:24
  348.3 0.0 copy-done.1
  348.3 6.6 %convolution_convert_fusion = bf16[256,1024]{1,0:T(8,128)(2,1)} fusion(bf16[256,4096]{0,1:T(8,128)(2,1)S(1)} %copy-done.1, bf16[1024,4096]{1,0:T(8,128)(2,1)} %all-gather.4.cloned.1.call-done), kind=kOutput, calls=%fused_computation.9 | convolution fusion | flops 2147745792 | bytes 11010048 | tf_op jit(solution)/shard_map/dot_general | solution.py:22
  (1 shorter events, 0.0 us)
Async XLA Ops:
  7.2 96.6 %all-gather.6.cloned.1.call-start = ((), (), s32[]{:S(2)}) async-start(), calls=%async_computation.3 | async-start | bytes 2621440 | tf_op jit(solution)/shard_map/all_gather | solution.py:30
  7.9 190.1 %reduce-scatter.2.cloned.1.call-start = ((), (), s32[]{:S(2)}) async-start(), calls=%async_computation.4 | async-start | bytes 4718592 | tf_op jit(solution)/shard_map/reduce_scatter | solution.py:35
  21.0 4.1 %copy-start.2 = (f32[4096]{0:T(1024)S(1)}, f32[4096]{0:T(1024)}, u32[]{:S(2)}) copy-start(f32[4096]{0:T(1024)} %param.13) | copy-start | bytes 49156
  21.0 4.1 %copy-start.3 = (f32[4096]{0:T(1024)S(1)}, f32[4096]{0:T(1024)}, u32[]{:S(2)}) copy-start(f32[4096]{0:T(1024)} %param.12) | copy-start | bytes 49156
  72.3 29.0 %copy-start = (bf16[256,4096]{0,1:T(8,128)(2,1)}, bf16[256,4096]{0,1:T(8,128)(2,1)S(1)}, u32[]{:S(2)}) copy-start(bf16[256,4096]{0,1:T(8,128)(2,1)S(1)} %fusion.3) | copy-start | bytes 6291460
  110.3 111.5 %all-gather.8.cloned.1.call-start = ((), (), s32[]{:S(2)}) async-start(), calls=%async_computation.5 | async-start | bytes 2621440 | tf_op jit(solution)/shard_map/all_gather | solution.py:36
  198.1 150.2 %all-gather.4.cloned.1.call-start = ((), (), s32[]{:S(2)}) async-start(), calls=%async_computation.2 | async-start | bytes 9437184 | tf_op jit(solution)/shard_map/all_gather | solution.py:24
  224.9 123.4 %copy-start.1 = (bf16[256,4096]{0,1:T(8,128)(2,1)S(1)}, bf16[256,4096]{0,1:T(8,128)(2,1)}, u32[]{:S(2)}) copy-start(bf16[256,4096]{0,1:T(8,128)(2,1)} %copy-done) | copy-start | bytes 6291460
Sparse Core Ops, SparseCore 0:
  9.5 25.2 all-gather.5
  110.4 87.5 reduce-scatter.1
  199.6 22.1 all-gather.7
  223.8 124.4 all-gather.3
where the time goes:
time: 362 us; the launch traced here: 361 us
  waiting for transfers between devices  232 us (64%)
  blocking collectives  71.3 us (20%)
  local copies, waits for them, and re-layouts  18.4 us (5%)
  between operations  13.8 us (4%)
  matrix products  13.1 us (4%)
  other arithmetic  12.1 us (3%)
    all_gather x1, waiting for transfers between devices, on_device(): lax.all_gather(weight_shard, 'fsdp', axis=0, tiled=True)  120 us
    reduce_scatter x1, waiting for transfers between devices, on_device(): lax.psum_scatter(unit_term, 'fsdp', scatter_dimension=0, tiled=True)  87.7 us
    psum x1, blocking collectives, on_device(): sum_plain, sum_cross = lax.psum((local_plain, local_cross), ('fsdp', 'dp'))  42.3 us
    all_to_all x1, blocking collectives, on_device(): lax.all_to_all(norm_grad, 'dp', split_axis=1, concat_axis=0, tiled=True)  29 us
    all_gather x1, waiting for transfers between devices, on_device(): summed = lax.all_gather(owner_part, 'dp', axis=1, tiled=True)  23.2 us
    unnamed x12, local copies, waits for them, and re-layouts  16.1 us
  transfers between devices with their start and end apart: 4, of which 3 were waited for; matrix products, arithmetic and copies ran while one was open for 8% of the time, Pallas kernels for 0%

commit v1 on v0

--- a/solution.py
+++ b/solution.py
@@ -33,7 +33,12 @@
         preferred_element_type=jnp.float32,
     )
     owner_part = lax.psum_scatter(unit_term, "fsdp", scatter_dimension=0, tiled=True)
-    summed = lax.all_gather(owner_part, "dp", axis=1, tiled=True)
+    ring = [owner_part]
+    for hop in range(3):
+        ring.append(lax.ppermute(ring[-1], "dp", [(dev, (dev + 1) % 4) for dev in range(4)]))
+    summed = jnp.roll(
+        jnp.concatenate(ring[::-1], axis=1), (lax.axis_index("dp") + 1) * ring[0].shape[1], axis=1
+    )
     rescale = 1.0 / math.sqrt(total_rows)
     return (grad_input, summed * rescale, sum_cross * rescale, sum_plain * rescale)
 

time: 362 us -> 339 us (0.936)
  waiting for transfers between devices: 232 us -> 209 us
    ppermute x0 -> x3, waiting for transfers between devices: none -> 26 us  [on_device(): lax.ppermute(ring[-1], 'dp', [(dev, (dev + 1) % 4) for dev in range(4)])]
    all_gather x1, waiting for transfers between devices: 120 us -> 94.4 us  [on_device(): lax.all_gather(weight_shard, 'fsdp', axis=0, tiled=True)]
    all_gather x1 -> x0, waiting for transfers between devices: 23.2 us -> none  [on_device(): summed = lax.all_gather(owner_part, 'dp', axis=1, tiled=True)]
    unnamed x12 -> x21, local copies, waits for them, and re-layouts: 16.1 us -> 18.5 us
  transfers between devices with their start and end apart: 4 -> 6, of which waited for: 3 -> 5; matrix products, arithmetic and copies ran while one was open for 8% -> 9% of each run, Pallas kernels for 0% -> 0%
where the time goes in v1:
time: 339 us
  waiting for transfers between devices  209 us (62%)
  blocking collectives  71.2 us (21%)
  local copies, waits for them, and re-layouts  20.9 us (6%)
  between operations  13.9 us (4%)
  matrix products  13.1 us (4%)
  other arithmetic  10.5 us (3%)
    all_gather x1, waiting for transfers between devices, on_device(): lax.all_gather(weight_shard, 'fsdp', axis=0, tiled=True)  94.4 us
    reduce_scatter x1, waiting for transfers between devices, on_device(): lax.psum_scatter(unit_term, 'fsdp', scatter_dimension=0, tiled=True)  87.1 us
    psum x1, blocking collectives, on_device(): sum_plain, sum_cross = lax.psum((local_plain, local_cross), ('fsdp', 'dp'))  42.2 us
    all_to_all x1, blocking collectives, on_device(): lax.all_to_all(norm_grad, 'dp', split_axis=1, concat_axis=0, tiled=True)  29 us
    ppermute x3, waiting for transfers between devices, on_device(): lax.ppermute(ring[-1], 'dp', [(dev, (dev + 1) % 4) for dev in range(4)])  26 us
    unnamed x21, local copies, waits for them, and re-layouts  18.5 us
  transfers between devices with their start and end apart: 6, of which 5 were waited for; matrix products, arithmetic and copies ran while one was open for 9% of the time, Pallas kernels for 0%

profile of v1, /device:TPU:0, one launch (start us, length us, event | category | flops | bytes accessed | tf_op | source)
XLA Modules:
  0.0 338.7 jit_solution(16744825231512493808)
XLA Ops:
  7.2 0.0 all-gather.5.cloned.1.call-start
  7.2 0.7 all-gather.5.cloned.1.call-update
  7.9 0.0 reduce-scatter.2.cloned.1.call-start
  7.9 3.3 copy.15
  11.2 5.6 %copy.14 = s32[256,4096]{0,1:T(8,128)} copy(s32[256,4096]{1,0:T(8,128)} %param.9) | data formatting | bytes 8388608 | tf_op args[2]
  16.8 4.1 %copy.13 = bf16[256,4096]{0,1:T(8,128)(2,1)} copy(bf16[256,4096]{1,0:T(8,128)(2,1)} %param.10) | data formatting | bytes 4194304 | tf_op args[3]
  21.0 0.0 copy-start.3
  21.0 0.0 copy-start.4
  21.0 4.1 %fusion.4 = (f32[4096]{0:T(1024)S(1)}, f32[4096]{0:T(1024)S(1)}) fusion(s32[256,4096]{0,1:T(8,128)} %copy.14, bf16[256,4096]{0,1:T(8,128)(2,1)} %copy.13, bf16[256,4096]{0,1:T(8,128)(2,1)S(1)} %copy.15), kind=kLoop, calls=%fused_computation.9 | loop fusion | flops 7331840 | bytes 8421376 | tf_op jit(solution)/shard_map/reduce_sum | solution.py:13
  25.0 0.0 copy-done.3
  25.0 0.0 copy-done.4
  25.1 42.2 %all-reduce = (f32[4096]{0:T(1024)S(1)}, f32[4096]{0:T(1024)S(1)}) all-reduce(f32[4096]{0:T(1024)S(1)} %get-tuple-element.17, f32[4096]{0:T(1024)S(1)} %get-tuple-element.16), channel_id=1, replica_groups=mesh['fsdp'=8,'dp'=4] {'fsdp','dp'}, use_global_device_ids=true, to_apply=%region_3.0 | all-reduce | flops 8192 | bytes 65536 | tf_op jit(solution)/shard_map/psum | solution.py:15
  67.3 0.6 broadcast_multiply_fusion
  67.9 4.3 %fusion.3 = bf16[256,4096]{0,1:T(8,128)(2,1)S(1)} fusion(bf16[256,4096]{0,1:T(8,128)(2,1)S(1)} %copy.15, f32[4096]{0:T(1024)S(1)} %get-tuple-element.24, f32[4096]{0:T(1024)S(1)} %get-tuple-element.21, f32[4096]{0:T(1024)S(1)} %mul.40, s32[256,4096]{0,1:T(8,128)} %copy.14, bf16[256,4096]{0,1:T(8,128)(2,1)} %copy.13), kind=kLoop, calls=%fused_computation.5 | loop fusion | flops 9437184 | bytes 10534912 | tf_op jit(solution)/shard_map/convert_element_type | solution.py:21
  72.2 0.0 copy-start
  72.2 1.3 copy-done
  73.5 29.0 %all_to_all.19 = bf16[256,4,1024]{0,2,1:T(8,128)(2,1)S(1)} all-to-all(bf16[256,4,1024]{0,2,1:T(8,128)(2,1)S(1)} %bitcast.9), channel_id=1, replica_groups=mesh['fsdp'=8,'dp'=4] {'dp'}, dimensions={1} | all-to-all | bytes 4194304 | tf_op jit(solution)/shard_map/all_to_all | solution.py:28
  102.6 2.4 copy.16
  104.9 0.0 all-gather.5.cloned.1.call-done
  104.9 6.6 %convolution_bitcast_fusion = f32[1024,1024]{0,1:T(8,128)} fusion(bf16[1024,1024]{1,0:T(8,128)(2,1)} %bitcast.11, bf16[1024,1024]{1,0:T(8,128)(2,1)} %all-gather.5.cloned.1.call-done), kind=kOutput, calls=%fused_computation.7 | convolution fusion | flops 2147483648 | bytes 8388608 | tf_op jit(solution)/shard_map/dot_general | solution.py:29
  111.5 0.0 reduce-scatter.2.cloned.1.call-update
  111.5 0.0 all-gather.3.cloned.1.call-start
  111.6 0.7 all-gather.3.cloned.1.call-update
  112.2 87.1 %reduce-scatter.2.cloned.1.call-done = f32[128,1024]{0,1:T(8,128)} async-done(((f32[1024,1024]{0,1:T(8,128)}), f32[128,1024]{0,1:T(8,128)}) %reduce-scatter.2.cloned.1.call-update) | async-done | bytes 524304 | tf_op jit(solution)/shard_map/reduce_scatter | solution.py:35
  199.4 0.0 copy-start.2
  199.4 0.0 collective-permute-start
  199.4 8.8 %collective-permute-done = f32[128,1024]{0,1:T(8,128)S(1)} collective-permute-done((f32[128,1024]{0,1:T(8,128)}, f32[128,1024]{0,1:T(8,128)S(1)}, u32[]{:S(2)}, u32[]{:S(2)}) %collective-permute-start) | collective-permute-done | bytes 524320 | tf_op jit(solution)/shard_map/ppermute | solution.py:38
  208.2 0.0 collective-permute-start.1
  208.2 8.6 %collective-permute-done.1 = f32[128,1024]{0,1:T(8,128)S(1)} collective-permute-done((f32[128,1024]{0,1:T(8,128)S(1)}, f32[128,1024]{0,1:T(8,128)S(1)}, u32[]{:S(2)}, u32[]{:S(2)}) %collective-permute-start.1) | collective-permute-done | bytes 524320 | tf_op jit(solution)/shard_map/ppermute | solution.py:38
  216.8 0.0 collective-permute-start.2
  216.8 8.6 %collective-permute-done.2 = f32[128,1024]{0,1:T(8,128)S(1)} collective-permute-done((f32[128,1024]{0,1:T(8,128)S(1)}, f32[128,1024]{0,1:T(8,128)S(1)}, u32[]{:S(2)}, u32[]{:S(2)}) %collective-permute-start.2) | collective-permute-done | bytes 524320 | tf_op jit(solution)/shard_map/ppermute | solution.py:38
  225.5 1.1 constant_dynamic-update-slice_fusion.4
  226.7 0.0 copy-done.2
  226.8 0.0 copy-start.1
  226.8 1.6 dynamic-slice_multiply_fusion
  228.4 2.9 copy.17
  231.2 94.4 %all-gather.3.cloned.1.call-done = bf16[1024,4096]{1,0:T(8,128)(2,1)} async-done(((bf16[128,4096]{1,0:T(8,128)(2,1)}), bf16[1024,4096]{1,0:T(8,128)(2,1)}) %all-gather.3.cloned.1.call-update) | async-done | bytes 8388624 | tf_op jit(solution)/shard_map/all_gather | solution.py:24
  325.6 0.0 copy-done.1
  325.6 6.6 %convolution_convert_fusion = bf16[256,1024]{1,0:T(8,128)(2,1)} fusion(bf16[256,4096]{0,1:T(8,128)(2,1)S(1)} %copy-done.1, bf16[1024,4096]{1,0:T(8,128)(2,1)} %all-gather.3.cloned.1.call-done), kind=kOutput, calls=%fused_computation.10 | convolution fusion | flops 2147745792 | bytes 11010048 | tf_op jit(solution)/shard_map/dot_general | solution.py:22
  (8 shorter events, 0.3 us)
Async XLA Ops:
  7.2 97.8 %all-gather.5.cloned.1.call-start = ((), (), s32[]{:S(2)}) async-start(), calls=%async_computation.3 | async-start | bytes 2621440 | tf_op jit(solution)/shard_map/all_gather | solution.py:30
  7.9 191.5 %reduce-scatter.2.cloned.1.call-start = ((), (), s32[]{:S(2)}) async-start(), calls=%async_computation.4 | async-start | bytes 4718592 | tf_op jit(solution)/shard_map/reduce_scatter | solution.py:35
  21.0 4.1 %copy-start.3 = (f32[4096]{0:T(1024)S(1)}, f32[4096]{0:T(1024)}, u32[]{:S(2)}) copy-start(f32[4096]{0:T(1024)} %param.13) | copy-start | bytes 49156
  21.0 4.1 %copy-start.4 = (f32[4096]{0:T(1024)S(1)}, f32[4096]{0:T(1024)}, u32[]{:S(2)}) copy-start(f32[4096]{0:T(1024)} %param.12) | copy-start | bytes 49156
  72.2 1.3 copy-start
  111.5 214.1 %all-gather.3.cloned.1.call-start = ((), (), s32[]{:S(2)}) async-start(), calls=%async_computation.2 | async-start | bytes 9437184 | tf_op jit(solution)/shard_map/all_gather | solution.py:24
  199.4 27.4 %copy-start.2 = (f32[128,1024]{0,1:T(8,128)S(1)}, f32[128,1024]{0,1:T(8,128)}, u32[]{:S(2)}) copy-start(f32[128,1024]{0,1:T(8,128)} %reduce-scatter.2.cloned.1.call-done) | copy-start | bytes 1572868
  199.4 8.8 %collective-permute-start = (f32[128,1024]{0,1:T(8,128)}, f32[128,1024]{0,1:T(8,128)S(1)}, u32[]{:S(2)}, u32[]{:S(2)}) collective-permute-start(f32[128,1024]{0,1:T(8,128)} %reduce-scatter.2.cloned.1.call-done), channel_id=1, source_target_pairs={{0,1},{1,2},{2,3},{3,0},{4,5},{5,6},{6,7},{7,4},{8,9},{9,10},{10,1... | collective-permute-start | bytes 1572872 | tf_op jit(solution)/shard_map/ppermute | solution.py:38
  208.2 8.6 %collective-permute-start.1 = (f32[128,1024]{0,1:T(8,128)S(1)}, f32[128,1024]{0,1:T(8,128)S(1)}, u32[]{:S(2)}, u32[]{:S(2)}) collective-permute-start(f32[128,1024]{0,1:T(8,128)S(1)} %collective-permute-done), channel_id=1, source_target_pairs={{0,1},{1,2},{2,3},{3,0},{4,5},{5,6},{6,7},{7,4},{8,9},{9,10},{10,1... | collective-permute-start | bytes 1572872 | tf_op jit(solution)/shard_map/ppermute | solution.py:38
  216.8 8.6 %collective-permute-start.2 = (f32[128,1024]{0,1:T(8,128)S(1)}, f32[128,1024]{0,1:T(8,128)S(1)}, u32[]{:S(2)}, u32[]{:S(2)}) collective-permute-start(f32[128,1024]{0,1:T(8,128)S(1)} %collective-permute-done.1), channel_id=1, source_target_pairs={{0,1},{1,2},{2,3},{3,0},{4,5},{5,6},{6,7},{7,4},{8,9},{9,10},{10,1... | collective-permute-start | bytes 1572872 | tf_op jit(solution)/shard_map/ppermute | solution.py:38
  226.8 98.8 %copy-start.1 = (bf16[256,4096]{0,1:T(8,128)(2,1)S(1)}, bf16[256,4096]{0,1:T(8,128)(2,1)}, u32[]{:S(2)}) copy-start(bf16[256,4096]{0,1:T(8,128)(2,1)} %copy-done) | copy-start | bytes 6291460
Sparse Core Ops, SparseCore 0:
  9.5 25.2 all-gather.4
  111.6 87.6 reduce-scatter.1
  201.5 124.0 all-gather.2
